TPU v7x, 32 devices: a whole 2x2x4 slice. The times are simulated.
32 devices in a mesh: seq: 8 (over z, y), head: 4 (over x, core).
Axes of the slice: x: 2, y: 2, z: 4, core: 2. Of those that a mesh axis runs over, the one named last changes fastest.
Arguments:
- tokens: bfloat16 [6144, 2560], P(('seq', 'head')), may hold values from -12 to 12
- pre_gain: float32 [2560], replicated, may hold values from 0.25 to 1.75
- inner_proj: bfloat16 [2560, 2, 5120], P(None, None, 'head'), may hold values from -0.125 to 0.125
- outer_proj: bfloat16 [2560, 336], replicated, may hold values from -0.125 to 0.125
- kernel_x: float32 [4, 5120], P(None, 'head'), may hold values from -3 to 3
- kernel_bc: float32 [4, 256], replicated, may hold values from -3 to 3
- offset_x: float32 [5120], P('head'), may hold values from -3 to 3
- offset_bc: float32 [256], replicated, may hold values from -3 to 3
- dt_bias: float32 [80], P('head'), may hold values from -7 to -5
- a_log: float32 [80], P('head'), may hold values from -12 to 4
- skip_gain: float32 [80], P('head'), may hold values from 0.5 to 1.5
- norm_gain: float32 [5120], P('head'), may hold values from 0.25 to 1.75
- out_proj: bfloat16 [5120, 2560], P('head'), may hold values from -0.078125 to 0.078125
Outputs:
- mixed: bfloat16 [6144, 2560], P(('seq', 'head'))
All inputs are finite; a program needn't handle non-finite values.
Results may differ from a plain program's by a relative error of at most 0.014.
Values may be sent and summed in bfloat16 or wider, within the bound.
A program may use at most 128 MiB of HBM per device.

v0:
```python
import functools

import jax
import jax.numpy as jnp
from jax import lax
from jax.experimental import pallas as pl
from jax.experimental.pallas import tpu as pltpu
from jax.sharding import PartitionSpec as P

SPAN = 256
HALO = 16
LANES = 128
PIECE = 512
CORES = 2


norm_floor = 0.1


def row_norm(row_block, gain_vector):
    widened = row_block.astype(jnp.float32)
    inverse_rms = lax.rsqrt(jnp.mean(widened * widened, axis=-1, keepdims=True) + norm_floor)
    return widened * inverse_rms * gain_vector


def silu(value):
    return value * (1.0 / (1.0 + jnp.exp(-value)))


def exact_dot(a, b):
    return jnp.dot(a, b, precision=lax.Precision.HIGHEST, preferred_element_type=jnp.float32)


def scan_kernel(
    sizes,
    inner_ref,
    bc_ref,
    dt_ref,
    kernel_x_ref,
    offset_x_ref,
    kernel_bc_ref,
    offset_bc_ref,
    rate_ref,
    skip_ref,
    gain_ref,
    proj_hbm,
    out_ref,
    proj,
    normed,
    pair_out,
    pair_in,
    keep,
    chip_out,
    chip_in,
    halo_x,
    halo_bc,
    ext_x,
    ext_bc,
    conv_x,
    conv_bc,
    y_buf,
    cum_buf,
    states,
    carried,
    sum_out,
    sum_in,
    rate_out,
    rate_in,
    carry_out,
    carry_in,
    sq_out,
    sq_in,
    halo_sems,
    sum_send,
    sum_recv,
    rate_send,
    rate_recv,
    carry_send,
    carry_recv,
    sq_send,
    sq_recv,
    proj_sem,
    pair_send,
    pair_recv,
    chip_send,
    chip_recv,
):
    devices, groups, rows, width, state, taps, head_size = sizes
    blocks = rows // SPAN
    share = state // devices
    total_width = width * groups
    me = lax.axis_index("seq")
    group = lax.axis_index("head")
    seq_peer = [lax.rem(me + o, devices) for o in range(devices)]
    seq_back = [lax.rem(me - o + devices, devices) for o in range(devices)]
    head_peer = [lax.rem(group + o, groups) for o in range(groups)]

    load_proj = pltpu.make_async_copy(proj_hbm, proj, proj_sem)
    load_proj.start()
    barrier = pltpu.get_barrier_semaphore()
    for o in range(1, devices):
        pl.semaphore_signal(barrier, 1, device_id={"seq": seq_peer[o]})
    for o in range(1, groups):
        pl.semaphore_signal(barrier, 1, device_id={"head": head_peer[o]})
    pl.semaphore_wait(barrier, devices + groups - 2)

    def remote(src, dst, send, recv, axis, peer):
        copy = pltpu.make_async_remote_copy(
            src_ref=src, dst_ref=dst, send_sem=send, recv_sem=recv, device_id={axis: peer}
        )
        return copy

    halo_copies = [
        remote(
            inner_ref.at[pl.ds(rows - HALO, HALO), pl.ds(width, width)],
            halo_x, halo_sems.at[0], halo_sems.at[1], "seq", seq_peer[1],
        ),
        remote(
            bc_ref.at[pl.ds(rows - HALO, HALO), :],
            halo_bc, halo_sems.at[2], halo_sems.at[3], "seq", seq_peer[1],
        ),
    ]
    for copy in halo_copies:
        copy.start()

    def widen(k, carry):
        row = pl.multiple_of(k * 64, 64)
        ext_x[pl.ds(8 + row, 64), :] = inner_ref[pl.ds(row, 64), pl.ds(width, width)].astype(
            jnp.float32
        )
        ext_bc[pl.ds(8 + row, 64), :] = bc_ref[pl.ds(row, 64), :].astype(jnp.float32)
        return carry

    lax.fori_loop(0, rows // 64, widen, 0)
    for copy in halo_copies:
        copy.wait()
    first = me > 0
    ext_x[0:8, :] = jnp.where(first, halo_x[...].astype(jnp.float32)[HALO - 8 :], 0.0)
    ext_bc[0:8, :] = jnp.where(first, halo_bc[...].astype(jnp.float32)[HALO - 8 :], 0.0)

    def convolve(source, weight, bias, target, columns):
        def step(k, carry):
            row = pl.multiple_of(k * 32, 32)
            for lower in range(0, columns, LANES):
                lanes = pl.ds(lower, LANES)
                window = source[pl.ds(row, 40), lanes]
                total = jnp.broadcast_to(bias[0:1, lanes], (32, LANES))
                for tap in range(taps):
                    shift = 8 - taps + 1 + tap
                    total = total + weight[tap : tap + 1, lanes] * window[shift : shift + 32]
                target[pl.ds(row, 32), lanes] = silu(total).astype(jnp.bfloat16)
            return carry

        lax.fori_loop(0, rows // 32, step, 0)

    convolve(ext_bc, kernel_bc_ref, offset_bc_ref, conv_bc, 2 * state)
    convolve(ext_x, kernel_x_ref, offset_x_ref, conv_x, width)

    head_of_lane = lax.broadcasted_iota(jnp.int32, (LANES, width), 1) // head_size
    spread = (head_of_lane == lax.broadcasted_iota(jnp.int32, (LANES, width), 0)).astype(
        jnp.float32
    )
    lower_tri = (
        lax.broadcasted_iota(jnp.int32, (SPAN, SPAN), 0)
        >= lax.broadcasted_iota(jnp.int32, (SPAN, SPAN), 1)
    ).astype(jnp.float32)

    states[0] = jnp.zeros((state, width), jnp.float32)
    prefix = jnp.zeros((1, LANES), jnp.float32)
    prefixes = []
    for block in range(blocks):
        span = pl.ds(block * SPAN, SPAN)
        step_sizes = dt_ref[span, :]
        running = exact_dot(lower_tri, step_sizes * rate_ref[...])
        cum_buf[span, :] = running
        last = running[SPAN - 1 : SPAN, :]
        end_weight = exact_dot(jnp.exp(last - running) * step_sizes, spread)
        scaled = (conv_x[span, :].astype(jnp.float32) * end_weight).astype(jnp.bfloat16)
        new_state = lax.dot_general(
            conv_bc[span, pl.ds(0, state)], scaled, (((0,), (0,)), ((), ())),
            preferred_element_type=jnp.float32,
        )
        decay = exact_dot(jnp.broadcast_to(jnp.exp(last), (8, LANES)), spread)[0:1]
        states[block + 1] = decay * states[block] + new_state
        prefixes.append(prefix)
        prefix = prefix + last

    for j in range(devices):
        sum_out[j] = states[blocks, pl.ds(j * share, share), :].astype(jnp.bfloat16)
    rate_out[...] = jnp.broadcast_to(prefix, (8, LANES))

    row_index = lax.broadcasted_iota(jnp.int32, (LANES, LANES), 0)
    col_index = lax.broadcasted_iota(jnp.int32, (LANES, LANES), 1)
    causal = row_index >= col_index
    lane_index = lax.broadcasted_iota(jnp.int32, (SPAN, LANES), 1)
    pair = LANES // head_size

    def inside(block):
        span = pl.ds(pl.multiple_of(block * SPAN, SPAN), SPAN)
        running = cum_buf[span, :]
        running_t = running.T
        steps_t = dt_ref[span, :].T
        scores = lax.dot_general(
            conv_bc[span, pl.ds(state, state)], conv_bc[span, pl.ds(0, state)],
            (((1,), (1,)), ((), ())), preferred_element_type=jnp.float32,
        )
        half = SPAN // 2
        for strip in range(width // LANES):
            lanes = pl.ds(strip * LANES, LANES)
            value = conv_x[span, lanes]
            upper, bottom, stacked_top, stacked = [], [], [], []
            for member in range(pair):
                head = strip * pair + member
                column = running[:, head : head + 1]
                line = running_t[head : head + 1, :]
                steps = steps_t[head : head + 1, :]

                def weights(r, c):
                    rs, cs = slice(r * half, (r + 1) * half), slice(c * half, (c + 1) * half)
                    gap = column[rs] - line[:, cs]
                    if r == c:
                        gap = jnp.where(causal, gap, -1e30)
                    return (scores[rs, cs] * jnp.exp(gap) * steps[:, cs]).astype(jnp.bfloat16)

                upper.append(weights(0, 0))
                bottom.extend([weights(1, 0), weights(1, 1)])
                own = jnp.where(lane_index // head_size == member, value, jnp.zeros_like(value))
                stacked_top.append(own[:half])
                stacked.append(own)
            top_out = jnp.dot(
                jnp.concatenate(upper, axis=1), jnp.concatenate(stacked_top, axis=0),
                preferred_element_type=jnp.float32,
            )
            bottom_out = jnp.dot(
                jnp.concatenate(bottom, axis=1), jnp.concatenate(stacked, axis=0),
                preferred_element_type=jnp.float32,
            )
            both = jnp.concatenate([top_out, bottom_out], axis=0)
            y_buf[span, lanes] = both + skip_ref[0:1, lanes] * value.astype(jnp.float32)

    sum_copies, rate_copies = [], []
    for o in range(1, devices):
        sum_copies.append(
            remote(
                sum_out.at[seq_peer[o]], sum_in.at[o], sum_send.at[o], sum_recv.at[o],
                "seq", seq_peer[o],
            )
        )
        rate_copies.append(
            remote(
                rate_out, rate_in.at[o], rate_send.at[o], rate_recv.at[o], "seq", seq_peer[o]
            )
        )
    for a, b in zip(sum_copies, rate_copies):
        b.start()
        a.start()

    early = max(blocks - 1, 1)

    def inside_step(block, carry):
        inside(block)
        return carry

    lax.fori_loop(0, early, inside_step, 0)

    for a, b in zip(sum_copies, rate_copies):
        b.wait()
        a.wait()
    sum_in[0] = sum_out[me]
    rate_in[0] = rate_out[...]

    running_state = jnp.zeros((share, width), jnp.float32)
    for i in range(devices):
        slot = lax.rem(me - i + devices, devices)
        carry_out[slot] = running_state.astype(jnp.bfloat16)
        decay = exact_dot(jnp.exp(rate_in[slot]), spread)[0:1]
        running_state = decay * running_state + sum_in[slot].astype(jnp.float32)

    carry_copies = []
    for o in range(1, devices):
        carry_copies.append(
            remote(
                carry_out.at[o], carry_in.at[o], carry_send.at[o], carry_recv.at[o],
                "seq", seq_back[o],
            )
        )
    for copy in carry_copies:
        copy.start()
    lax.fori_loop(early, blocks, inside_step, 0)
    for copy in carry_copies:
        copy.wait()
    carry_in[0] = carry_out[0]
    for j in range(devices):
        slot = lax.rem(j - me + devices, devices)
        carried[pl.ds(j * share, share), :] = carry_in[slot].astype(jnp.float32)

    squares = []
    for block in range(blocks):
        span = pl.ds(block * SPAN, SPAN)
        entry_decay = exact_dot(
            jnp.broadcast_to(jnp.exp(prefixes[block]), (8, LANES)), spread
        )[0:1]
        entering = (states[block] + entry_decay * carried[...]).astype(jnp.bfloat16)
        growth = jnp.exp(cum_buf[span, :])
        partial_sum = jnp.zeros((SPAN, LANES), jnp.float32)
        for strip in range(width // LANES):
            lanes = pl.ds(strip * LANES, LANES)
            column = slice(strip * LANES, (strip + 1) * LANES)
            cross = jnp.dot(
                conv_bc[span, pl.ds(state, state)], entering[:, column],
                preferred_element_type=jnp.float32,
            )
            scale = exact_dot(growth, spread[:, column])
            gated = (y_buf[span, lanes] + scale * cross) * silu(
                inner_ref[span, lanes].astype(jnp.float32)
            )
            y_buf[span, lanes] = gated
            partial_sum = partial_sum + gated * gated
        squares.append(jnp.sum(partial_sum.T, axis=0, keepdims=True))
    own_squares = jnp.concatenate(squares, axis=1)
    sq_out[...] = jnp.broadcast_to(own_squares, (8, rows))
    sq_copies = []
    for o in range(1, groups):
        sq_copies.append(
            remote(sq_out, sq_in.at[o], sq_send.at[o], sq_recv.at[o], "head", head_peer[o])
        )
    for copy in sq_copies:
        copy.start()
    for copy in sq_copies:
        copy.wait()
    total = own_squares
    for o in range(1, groups):
        total = total + sq_in[o, 0:1, :]
    inverse = lax.rsqrt(total / total_width + norm_floor)
    for block in range(blocks):
        part = jnp.broadcast_to(inverse[:, block * SPAN : (block + 1) * SPAN], (LANES, SPAN)).T
        span = pl.ds(block * SPAN, SPAN)
        for strip in range(width // LANES):
            lanes = pl.ds(strip * LANES, LANES)
            normed[span, lanes] = (y_buf[span, lanes] * part * gain_ref[0:1, lanes]).astype(
                jnp.bfloat16
            )

    load_proj.wait()
    own_rows = rows // groups
    chips = groups // CORES
    chip, core = group // CORES, lax.rem(group, CORES)
    partner = group + 1 - 2 * core
    pieces = proj.shape[1] // PIECE
    jobs = [(o, q) for o in list(range(1, chips)) + [0] for q in range(pieces)]

    def pair_copy(o, q):
        return remote(
            pair_out.at[o, q], pair_in.at[o, q], pair_send.at[o, q], pair_recv.at[o, q],
            "head", partner,
        )

    def chip_copy(o, q):
        target = lax.rem(chip + o, chips) * CORES + core
        return remote(
            chip_out.at[o, q], chip_in.at[o, q], chip_send.at[o, q], chip_recv.at[o, q],
            "head", target,
        )

    def start_job(o, q):
        base = pl.multiple_of(lax.rem(chip + o, chips) * CORES * own_rows, own_rows)
        columns = pl.ds(q * PIECE, PIECE)
        theirs = pl.ds(pl.multiple_of(base + (1 - core) * own_rows, own_rows), own_rows)
        mine = pl.ds(pl.multiple_of(base + core * own_rows, own_rows), own_rows)
        pair_out[o, q] = jnp.dot(
            normed[theirs, :], proj[:, columns], preferred_element_type=jnp.float32
        ).astype(jnp.bfloat16)
        pair_copy(o, q).start()
        keep[o, q] = jnp.dot(
            normed[mine, :], proj[:, columns], preferred_element_type=jnp.float32
        )

    def finish_job(o, q):
        pair_copy(o, q).wait()
        if o > 0:
            chip_out[o, q] = (keep[o, q] + pair_in[o, q].astype(jnp.float32)).astype(jnp.bfloat16)
            chip_copy(o, q).start()

    for index, job in enumerate(jobs):
        start_job(*job)
        if index > 0:
            finish_job(*jobs[index - 1])
    finish_job(*jobs[-1])
    for q in range(pieces):
        result = keep[0, q] + pair_in[0, q].astype(jnp.float32)
        for o in range(1, chips):
            chip_copy(o, q).wait()
            result = result + chip_in[o, q].astype(jnp.float32)
        out_ref[:, pl.ds(q * PIECE, PIECE)] = result.astype(jnp.bfloat16)


def scan_call(inner, bc, step_sizes, kernel_x, offset_x, kernel_bc, offset_bc, rate, skip, gain, proj, head_size):
    devices, groups = lax.axis_size("seq"), lax.axis_size("head")
    rows, width = inner.shape[0], kernel_x.shape[1]
    state, taps = bc.shape[1] // 2, kernel_x.shape[0]
    blocks, share = rows // SPAN, state // devices
    own_rows, model, chips = rows // groups, proj.shape[1], groups // CORES
    pieces = model // PIECE
    sizes = (devices, groups, rows, width, state, taps, head_size)
    f32, bf16 = jnp.float32, jnp.bfloat16
    sem = pltpu.SemaphoreType.DMA
    return pl.pallas_call(
        functools.partial(scan_kernel, sizes),
        out_shape=jax.ShapeDtypeStruct((own_rows, model), bf16),
        in_specs=[pl.BlockSpec(memory_space=pltpu.VMEM)] * 10
        + [pl.BlockSpec(memory_space=pl.ANY)],
        out_specs=pl.BlockSpec(memory_space=pltpu.VMEM),
        scratch_shapes=[
            pltpu.VMEM(proj.shape, bf16),
            pltpu.VMEM((rows, width), bf16),
            pltpu.VMEM((chips, pieces, own_rows, PIECE), bf16),
            pltpu.VMEM((chips, pieces, own_rows, PIECE), bf16),
            pltpu.VMEM((chips, pieces, own_rows, PIECE), f32),
            pltpu.VMEM((chips, pieces, own_rows, PIECE), bf16),
            pltpu.VMEM((chips, pieces, own_rows, PIECE), bf16),
            pltpu.VMEM((HALO, width), bf16),
            pltpu.VMEM((HALO, 2 * state), bf16),
            pltpu.VMEM((rows + 8, width), f32),
            pltpu.VMEM((rows + 8, 2 * state), f32),
            pltpu.VMEM((rows, width), bf16),
            pltpu.VMEM((rows, 2 * state), bf16),
            pltpu.VMEM((rows, width), f32),
            pltpu.VMEM((rows, LANES), f32),
            pltpu.VMEM((blocks + 1, state, width), f32),
            pltpu.VMEM((state, width), f32),
            pltpu.VMEM((devices, share, width), bf16),
            pltpu.VMEM((devices, share, width), bf16),
            pltpu.VMEM((8, LANES), f32),
            pltpu.VMEM((devices, 8, LANES), f32),
            pltpu.VMEM((devices, share, width), bf16),
            pltpu.VMEM((devices, share, width), bf16),
            pltpu.VMEM((8, rows), f32),
            pltpu.VMEM((groups, 8, rows), f32),
            sem((4,)),
            sem((devices,)),
            sem((devices,)),
            sem((devices,)),
            sem((devices,)),
            sem((devices,)),
            sem((devices,)),
            sem((groups,)),
            sem((groups,)),
            sem,
            sem((chips, pieces)),
            sem((chips, pieces)),
            sem((chips, pieces)),
            sem((chips, pieces)),
        ],
        compiler_params=pltpu.CompilerParams(
            collective_id=0, has_side_effects=True, vmem_limit_bytes=60 * 1024 * 1024
        ),
    )(inner, bc, step_sizes, kernel_x, offset_x, kernel_bc, offset_bc, rate, skip, gain, proj)


def on_device(
    tokens,
    pre_gain,
    inner_proj,
    outer_proj,
    kernel_x,
    kernel_bc,
    offset_x,
    offset_bc,
    dt_bias,
    a_log,
    skip_gain,
    norm_gain,
    out_proj,
):
    model_width = inner_proj.shape[0]
    local_width = inner_proj.shape[2]
    head_count = dt_bias.shape[0]
    head_size = local_width // head_count
    state_size = kernel_bc.shape[1] // 2
    joined_proj = inner_proj.reshape(model_width, 2 * local_width)
    normed = row_norm(lax.all_gather(tokens, "head", axis=0, tiled=True), pre_gain).astype(
        jnp.bfloat16
    )
    inner_part = jnp.dot(normed, joined_proj, preferred_element_type=jnp.float32).astype(
        jnp.bfloat16
    )
    outer_part = jnp.dot(normed, outer_proj, preferred_element_type=jnp.float32)
    head_index = lax.axis_index("head")
    dt_raw = lax.dynamic_slice_in_dim(
        outer_part, 2 * state_size + head_index * head_count, head_count, 1
    )
    lane_pad = LANES - head_count
    step_sizes = jnp.pad(jax.nn.softplus(dt_raw + dt_bias), ((0, 0), (0, lane_pad)))
    rate = jnp.pad(-jnp.exp(a_log), (0, lane_pad))[None]
    return scan_call(
        inner_part,
        outer_part[:, : 2 * state_size].astype(jnp.bfloat16),
        step_sizes,
        kernel_x,
        offset_x[None],
        kernel_bc,
        offset_bc[None],
        rate,
        jnp.repeat(skip_gain, head_size)[None],
        norm_gain[None],
        out_proj,
        head_size,
    )


def solution(mesh):
    return jax.shard_map(
        on_device,
        mesh=mesh,
        in_specs=(
            P(("seq", "head"), None),
            P(),
            P(None, None, "head"),
            P(),
            P(None, "head"),
            P(),
            P("head"),
            P(),
            P("head"),
            P("head"),
            P("head"),
            P("head"),
            P("head", None),
        ),
        out_specs=P(("seq", "head"), None),
        check_vma=False,
    )
```

profile of v0, /device:TPU:0, one launch (start us, length us, event | category | flops | bytes accessed | tf_op | source)
XLA Modules:
  0.0 154.7 jit_solution(7435253350966145324)
XLA Ops:
  6.5 0.0 copy-start
  6.5 0.0 all-gather.2.cloned.1.call-start
  6.5 0.7 all-gather.2.cloned.1.call-update
  7.3 0.0 copy-start.1
  7.3 0.0 copy-start.3
  7.3 0.0 copy-start.2
  7.3 0.0 copy-start.6
  7.3 0.0 copy-start.5
  7.3 12.4 %copy.20 = bf16[320,8,2,1280]{3,1,2,0:T(8,128)(2,1)} copy(bf16[320,8,2,1280]{3,2,1,0:T(2,128)(2,1)} %bitcast.7) | data formatting | bytes 26214400
  19.8 0.0 copy-done.1
  19.8 0.6 broadcast_in_dim.18.offset_x_ref
  20.4 0.0 copy-done.3
  20.4 0.1 broadcast_in_dim.21
  20.4 0.7 broadcast_in_dim_reshape.3.skip_ref
  21.1 0.0 copy-done.2
  21.1 0.6 broadcast_in_dim.22.gain_ref
  21.7 0.0 copy-done.6
  21.7 0.6 pad_bitcast_fusion.rate_ref
  22.3 22.3 %all-gather.2.cloned.1.call-done = bf16[768,2560]{1,0:T(8,128)(2,1)} async-done(((bf16[192,2560]{1,0:T(8,128)(2,1)}), bf16[768,2560]{1,0:T(8,128)(2,1)}) %all-gather.2.cloned.1.call-update) | async-done | bytes 3932176 | tf_op jit(solution)/shard_map/all_gather | solution.py:481
  44.6 2.9 %fusion = f32[768]{0:T(1024)S(1)} fusion(bf16[768,2560]{1,0:T(8,128)(2,1)} %all-gather.2.cloned.1.call-done), kind=kLoop, calls=%fused_computation.2 | loop fusion | flops 5897472 | bytes 3935232 | tf_op jit(solution)/shard_map/reduce_sum | solution.py:22
  47.6 0.0 copy-start.4
  47.6 0.0 copy-done
  47.6 0.0 copy-done.5
  47.6 3.7 %fusion.3 = f32[768,336]{0,1:T(8,128)S(1)} fusion(bf16[2560,336]{0,1:T(8,128)(2,1)S(1)} %copy-done, bf16[768,2560]{1,0:T(8,128)(2,1)} %all-gather.2.cloned.1.call-done, f32[2560]{0:T(1024)S(1)} %copy-done.5, f32[768]{0:T(1024)S(1)} %add_rsqrt_fusion), kind=kOutput, calls=%fused_computation.7 | convolution fusion | flops 1329070080 | bytes 6697984 | tf_op jit(solution)/shard_map/dot_general | solution.py:487
  51.4 0.9 copy.18.bc_ref
  52.3 0.2 copy.19
  52.5 0.0 copy-done.4
  52.5 0.2 compare_select_fusion
  52.7 0.8 pad.8.dt_ref
  53.5 15.9 %convolution_convert_fusion.inner_ref = bf16[768,2560]{1,0:T(8,128)(2,1)} fusion(bf16[2560,2560]{1,0:T(8,128)(2,1)} %bitcast.8, bf16[768,2560]{1,0:T(8,128)(2,1)} %all-gather.2.cloned.1.call-done, f32[2560]{0:T(1024)S(1)} %copy-done.5, f32[768]{0:T(1024)S(1)} %add_rsqrt_fusion), kind=kOutput, calls=%fused_computation.5 | convolution fusion | flops 10076160000 | bytes 20984832 | tf_op jit(solution)/shard_map/dot_general | solution.py:484
  69.4 76.2 %shard_map.127 = bf16[192,2560]{1,0:T(8,128)(2,1)} custom-call(bf16[768,2560]{1,0:T(8,128)(2,1)} %convolution_convert_fusion.inner_ref, bf16[768,256]{1,0:T(8,128)(2,1)} %copy.18.bc_ref, f32[768,128]{1,0:T(8,128)} %pad.8.dt_ref, f32[4,1280]{1,0:T(4,128)} %kernel_x_ref.1, f32[1,1280]{1,0:T(1,128)} %broadcast_in_dim.18.offset_x_ref, f32[4,256]{1,0:T(4,128)} %kernel_bc_ref.1, ...), custom_call_target="tpu_custom_call" | custom-call | tf_op jit(solution)/shard_map/pallas_call | solution.py:407
  145.6 2.2 %copy.22 = bf16[192,2560]{1,0:T(8,128)(2,1)} copy(bf16[192,2560]{1,0:T(8,128)(2,1)} %shard_map.127) | data formatting | bytes 1966080
  (4 shorter events, 0.1 us)
Async XLA Ops:
  6.5 41.1 %copy-start = (bf16[2560,336]{0,1:T(8,128)(2,1)S(1)}, bf16[2560,336]{0,1:T(8,128)(2,1)}, u32[]{:S(2)}) copy-start(bf16[2560,336]{0,1:T(8,128)(2,1)} %param.16) | copy-start | bytes 5160964
  6.5 38.1 %all-gather.2.cloned.1.call-start = ((), (), s32[]{:S(2)}) async-start(), calls=%async_computation | async-start | bytes 4915200 | tf_op jit(solution)/shard_map/all_gather | solution.py:481
  7.3 12.5 %copy-start.1 = (f32[1280]{0:T(1024)S(1)}, f32[1280]{0:T(1024)}, u32[]{:S(2)}) copy-start(f32[1280]{0:T(1024)} %param.19) | copy-start | bytes 15364
  7.3 13.1 %copy-start.3 = (f32[20]{0:T(128)S(1)}, f32[20]{0:T(128)}, u32[]{:S(2)}) copy-start(f32[20]{0:T(128)} %param.23) | copy-start | bytes 244
  7.3 13.8 %copy-start.2 = (f32[1280]{0:T(1024)S(1)}, f32[1280]{0:T(1024)}, u32[]{:S(2)}) copy-start(f32[1280]{0:T(1024)} %param.24) | copy-start | bytes 15364
  7.3 14.4 %copy-start.6 = (f32[20]{0:T(128)S(1)}, f32[20]{0:T(128)}, u32[]{:S(2)}) copy-start(f32[20]{0:T(128)} %param.22) | copy-start | bytes 244
  7.3 40.3 %copy-start.5 = (f32[2560]{0:T(1024)S(1)}, f32[2560]{0:T(1024)}, u32[]{:S(2)}) copy-start(f32[2560]{0:T(1024)} %param.14) | copy-start | bytes 30724
  47.6 4.9 %copy-start.4 = (f32[20]{0:T(128)S(1)}, f32[20]{0:T(128)}, u32[]{:S(2)}) copy-start(f32[20]{0:T(128)} %param.21) | copy-start | bytes 244
Sparse Core Ops, SparseCore 0:
  8.9 35.6 all-gather.1
where the time goes:
time: 155 us
  Pallas kernels  76.2 us (49%)
  waiting for transfers between devices  23 us (15%)
  matrix products  19.6 us (13%)
  local copies, waits for them, and re-layouts  19.1 us (12%)
  between operations  13.5 us (9%)
  other arithmetic  3.18 us (2%)
    pallas_call x1, Pallas kernels, scan_call(): pl.pallas_call(functools.partial(scan_kernel, sizes), out_shape=jax.Shape...  76.2 us
    all_gather x1, waiting for transfers between devices, on_device(): lax.all_gather(tokens, 'head', axis=0, tiled=True)  22.3 us
    dot_general x1, matrix products, on_device(): jnp.dot(normed, joined_proj, preferred_element_type=jnp.float32)  15.9 us
    unnamed x18, local copies, waits for them, and re-layouts  15.8 us
    dot_general x1, matrix products, on_device(): outer_part = jnp.dot(normed, outer_proj, preferred_element_type=jnp.float32)  3.72 us
  transfers between devices with their start and end apart: 1, of which 1 were waited for; matrix products, arithmetic and copies ran while one was open for 10% of the time, Pallas kernels for 0%

commit v1 on v0

v1 whole, which is shorter than its diff:
```python
import functools

import jax
import jax.numpy as jnp
from jax import lax
from jax.experimental import pallas as pl
from jax.experimental.pallas import tpu as pltpu
from jax.sharding import PartitionSpec as P

SPAN = 256
HALO = 8
LANES = 128
PIECE = 512
CORES = 2
FEED = 512
DEPTH = 256

norm_floor = 0.1


def silu(value):
    half = 0.5 * value
    return half * jnp.tanh(half) + half


def softplus(value):
    small = jnp.exp(-jnp.abs(value))
    series = small * (1.0 - small * (0.5 - small * (1.0 / 3.0 - small * 0.25)))
    return jnp.maximum(value, 0.0) + jnp.where(small < 0.03, series, jnp.log(1.0 + small))


def in_two(value):
    top = value.astype(jnp.bfloat16)
    return top, (value - top.astype(jnp.float32)).astype(jnp.bfloat16)


def in_three(value):
    top = value.astype(jnp.bfloat16)
    rest = value - top.astype(jnp.float32)
    middle = rest.astype(jnp.bfloat16)
    return top, middle, (rest - middle.astype(jnp.float32)).astype(jnp.bfloat16)


def layer_kernel(
    sizes,
    tokens_hbm,
    pre_gain_ref,
    inner_hbm,
    outer_hbm,
    kernel_x_ref,
    kernel_bc_ref,
    offset_x_ref,
    offset_bc_ref,
    dt_bias_ref,
    a_log_ref,
    skip_gain_ref,
    norm_gain_ref,
    proj_hbm,
    out_ref,
    tok,
    tok_in,
    raw,
    gate_w,
    inner_w,
    outer_w,
    proj,
    gate,
    ext_x,
    ext_bc,
    dt_buf,
    halo_x,
    halo_bc,
    halo_x_out,
    halo_bc_out,
    conv_x,
    conv_bc,
    y_buf,
    cum_buf,
    states,
    carried,
    sum_out,
    sum_in,
    rate_out,
    rate_in,
    carry_out,
    carry_in,
    normed,
    sq_out,
    sq_in,
    inv_col,
    pair_out,
    pair_in,
    chip_out,
    chip_in,
    keep,
    small,
    tok_sem,
    raw_sems,
    load_sems,
    row_send,
    row_recv,
    mate_send,
    mate_recv,
    halo_sems,
    sum_send,
    sum_recv,
    rate_send,
    rate_recv,
    carry_send,
    carry_recv,
    sq_send,
    sq_recv,
    pair_send,
    pair_recv,
    chip_send,
    chip_recv,
):
    devices, groups, rows, model, width, state, taps, head_count = sizes
    f32, bf16 = jnp.float32, jnp.bfloat16
    head_size = width // head_count
    blocks = rows // SPAN
    share = state // devices
    total_width = width * groups
    own_rows = rows // groups
    chips = groups // CORES
    chip_rows = own_rows * CORES
    feeds = model // FEED
    steps = model // DEPTH
    strips = width // LANES
    me = lax.axis_index("seq")
    group = lax.axis_index("head")
    chip, core = group // CORES, lax.rem(group, CORES)
    partner = group + 1 - 2 * core
    seq_peer = [lax.rem(me + o, devices) for o in range(devices)]
    seq_back = [lax.rem(me - o + devices, devices) for o in range(devices)]
    head_peer = [lax.rem(group + o, groups) for o in range(groups)]

    def remote(src, dst, send, recv, axis, peer):
        return pltpu.make_async_remote_copy(
            src_ref=src, dst_ref=dst, send_sem=send, recv_sem=recv, device_id={axis: peer}
        )

    own = pl.ds(pl.multiple_of(group * own_rows, 16), own_rows)
    load_tok = pltpu.make_async_copy(tokens_hbm, tok_in, tok_sem)
    load_tok.start()

    def raw_copy(step, slot, strip):
        return pltpu.make_async_copy(
            inner_hbm.at[pl.ds(pl.multiple_of(step * DEPTH, DEPTH), DEPTH), :, pl.ds(strip * LANES, LANES)],
            raw.at[slot, strip],
            raw_sems.at[slot, strip],
        )

    for strip in range(strips):
        raw_copy(0, 0, strip).start()
    load_outer = pltpu.make_async_copy(outer_hbm, outer_w, load_sems.at[0])
    load_outer.start()
    for strip in range(strips):
        raw_copy(1, 1, strip).start()
    load_proj = pltpu.make_async_copy(proj_hbm, proj, load_sems.at[1])

    barrier = pltpu.get_barrier_semaphore()
    for o in range(1, devices):
        pl.semaphore_signal(barrier, 1, device_id={"seq": seq_peer[o]})
    for o in range(1, groups):
        pl.semaphore_signal(barrier, 1, device_id={"head": head_peer[o]})

    small[...] = jnp.zeros_like(small)
    small[0:1, 0:head_count] = dt_bias_ref[...].reshape(1, head_count)
    small[1:2, 0:head_count] = -jnp.exp(a_log_ref[...].reshape(1, head_count))
    small[2:3, 0:head_count] = skip_gain_ref[...].reshape(1, head_count)

    def clear(k, carry):
        row = pl.multiple_of(k * 64, 64)
        gate[pl.ds(row, 64), :] = jnp.zeros((64, width), f32)
        ext_x[pl.ds(8 + row, 64), :] = jnp.zeros((64, width), f32)
        ext_bc[pl.ds(8 + row, 64), :] = jnp.zeros((64, 2 * state), f32)
        dt_buf[pl.ds(row, 64), :] = jnp.zeros((64, LANES), f32)
        return carry

    def normalise(k, carry):
        row = pl.multiple_of(k * 16, 16)
        squares = jnp.zeros((16, LANES), f32)
        for column in range(0, model, LANES):
            value = tok_in[pl.ds(row, 16), pl.ds(column, LANES)].astype(f32)
            squares = squares + value * value
        inverse = lax.rsqrt(jnp.sum(squares, axis=1, keepdims=True) / model + norm_floor)
        for column in range(0, model, LANES):
            lanes = pl.ds(column, LANES)
            value = tok_in[pl.ds(row, 16), lanes].astype(f32)
            tok[pl.ds(pl.multiple_of(group * own_rows + row, 16), 16), lanes] = (
                value * inverse * pre_gain_ref[lanes].reshape(1, LANES)
            ).astype(bf16)
        return carry

    load_tok.wait()
    lax.fori_loop(0, own_rows // 16, normalise, 0)
    pl.semaphore_wait(barrier, devices + groups - 2)

    def feed_at(chip_index, core_index, feed):
        begin = pl.multiple_of((chip_index * CORES + core_index) * own_rows, 16)
        return tok.at[pl.ds(begin, own_rows), pl.ds(pl.multiple_of(feed * FEED, FEED), FEED)]

    def mate_copy(o, feed):
        piece = feed_at(lax.rem(chip - o + chips, chips), core, feed)
        return remote(piece, piece, mate_send.at[o, feed], mate_recv.at[o, feed], "head", partner)

    def row_copy(o, feed):
        piece = feed_at(chip, core, feed)
        target = lax.rem(chip + o, chips) * CORES + core
        return remote(piece, piece, row_send.at[o, feed], row_recv.at[o, feed], "head", target)

    for feed in range(feeds):
        for o in range(1, chips):
            row_copy(o, feed).start()
    for feed in range(feeds):
        mate_copy(0, feed).start()
    lax.fori_loop(0, rows // 64, clear, 0)

    out_row = lax.broadcasted_iota(jnp.int32, (DEPTH, DEPTH), 0)
    in_row = lax.broadcasted_iota(jnp.int32, (DEPTH, DEPTH), 1)
    half_depth = DEPTH // 2
    parting = (
        in_row == jnp.where(out_row < half_depth, 2 * out_row, 2 * (out_row - half_depth) + 1)
    ).astype(f32).astype(bf16)

    def separate(step, slot):
        for lower in range(0, strips, 2):
            members = range(lower, min(lower + 2, strips))
            columns = pl.ds(lower * LANES, len(members) * LANES)
            for part in range(2):
                parts = [
                    raw.at[slot, m].reshape(2 * DEPTH, LANES)[pl.ds(part * DEPTH, DEPTH), :]
                    for m in members
                ]
                both = jnp.dot(
                    parting, jnp.concatenate(parts, axis=1), preferred_element_type=f32
                ).astype(bf16)
                begin = pl.multiple_of(step * DEPTH + part * half_depth, half_depth)
                gate_w[pl.ds(begin, half_depth), columns] = both[:half_depth]
                inner_w[pl.ds(begin, half_depth), columns] = both[half_depth:]

    tile = 256 if width % 256 == 0 else LANES

    def rows_of(base, begin, depth):
        return tok[pl.ds(pl.multiple_of(base, 16), chip_rows), pl.ds(begin, depth)]

    def gather_into(target, offset, base, weight, begin, depth):
        here = pl.ds(pl.multiple_of(base + offset, 8), chip_rows)
        for column in range(0, width, tile):
            columns = pl.ds(column, tile)
            target[here, columns] += jnp.dot(
                rows_of(base, begin, depth), weight[pl.ds(begin, depth), columns],
                preferred_element_type=f32,
            )

    def gather_outer(base, begin, depth):
        result = lax.dot_general(
            rows_of(base, begin, depth), outer_w[:, pl.ds(begin, depth)], (((1,), (1,)), ((), ())),
            preferred_element_type=f32,
        )
        ext_bc[pl.ds(pl.multiple_of(base + 8, 8), chip_rows), :] += result[:, : 2 * state]
        raw_columns = result.shape[1] - 2 * state
        dt_buf[pl.ds(pl.multiple_of(base, 8), chip_rows), pl.ds(0, raw_columns)] += result[:, 2 * state :]

    local_base = pl.multiple_of(chip * chip_rows, 32)
    load_outer.wait()

    def local_step(step, carry):
        slot = lax.rem(step, 2)
        for strip in range(strips):
            raw_copy(step, slot, strip).wait()
        separate(step, slot)

        @pl.when(step + 2 < steps)
        def _():
            for strip in range(strips):
                raw_copy(step + 2, slot, strip).start()

        @pl.when(lax.rem(step, FEED // DEPTH) == 0)
        def _():
            mate_copy(0, step // (FEED // DEPTH)).wait_recv()

        begin = pl.multiple_of(step * DEPTH, DEPTH)
        gather_into(ext_x, 8, local_base, inner_w, begin, DEPTH)
        gather_outer(local_base, begin, DEPTH)
        gather_into(gate, 0, local_base, gate_w, begin, DEPTH)
        return carry

    lax.fori_loop(0, steps, local_step, 0)
    load_proj.start()

    bias_row, rate_row = small[0:1, :], small[1:2, :]
    own_lane = lax.broadcasted_iota(jnp.int32, (32, LANES), 1) < head_count

    def finish_rows(base):
        def step(k, carry):
            row = pl.multiple_of(base + k * 32, 32)
            here, lower = pl.ds(row, 32), pl.ds(row + 8, 32)
            for target, columns in ((ext_x, width), (ext_bc, 2 * state)):
                for column in range(0, columns, LANES):
                    lanes = pl.ds(column, LANES)
                    target[lower, lanes] = target[lower, lanes].astype(bf16).astype(f32)
            raw_steps = pltpu.roll(dt_buf[here, :], lax.rem(LANES - group * head_count, LANES), 1)
            dt_buf[here, :] = jnp.where(own_lane, softplus(raw_steps + bias_row), 0.0)
            return carry

        lax.fori_loop(0, chip_rows // 32, step, 0)

    def finish_gate(base):
        def step(k, carry):
            here = pl.ds(pl.multiple_of(base + k * 32, 32), 32)
            for column in range(0, width, LANES):
                lanes = pl.ds(column, LANES)
                gate[here, lanes] = silu(gate[here, lanes].astype(bf16).astype(f32))
            return carry

        lax.fori_loop(0, chip_rows // 32, step, 0)

    def convolve(source, weight, bias, target, columns, row):
        for lower in range(0, columns, LANES):
            lanes = pl.ds(lower, LANES)
            window = source[pl.ds(row, 40), lanes]
            total = jnp.broadcast_to(bias[lanes].reshape(1, LANES), (32, LANES))
            for tap in range(taps):
                shift = 8 - taps + 1 + tap
                total = total + weight[tap : tap + 1, lanes] * window[shift : shift + 32]
            target[pl.ds(row, 32), lanes] = silu(total).astype(bf16)

    def convolve_rows(begin, first, last):
        def step(k, carry):
            row = pl.multiple_of(begin + k * 32, 32)
            convolve(ext_bc, kernel_bc_ref, offset_bc_ref, conv_bc, 2 * state, row)
            convolve(ext_x, kernel_x_ref, offset_x_ref, conv_x, width, row)
            return carry

        lax.fori_loop(first, last, step, 0)

    finish_rows(local_base)
    convolve_rows(local_base, 1, chip_rows // 32)

    def far_base(o):
        return pl.multiple_of(lax.rem(chip - o + chips, chips) * chip_rows, 32)

    def take_feed(o, feed):
        row_copy(o, feed).wait_recv()
        mate_copy(o, feed).start()

    def far_step(o, feed):
        mate_copy(o, feed).wait_recv()
        begin = pl.multiple_of(feed * FEED, FEED)
        gather_into(ext_x, 8, far_base(o), inner_w, begin, FEED)
        gather_outer(far_base(o), begin, FEED)

    def far_gate(o, feed):
        gather_into(gate, 0, far_base(o), gate_w, pl.multiple_of(feed * FEED, FEED), FEED)

    for o in range(1, chips):
        take_feed(o, 0)

        def far_loop(feed, carry):
            take_feed(o, feed + 1)
            far_step(o, feed)
            far_gate(o, feed)
            return carry

        lax.fori_loop(0, feeds - 1, far_loop, 0)
        far_step(o, feeds - 1)
        finish_rows(far_base(o))
        if o < chips - 1:
            far_gate(o, feeds - 1)

    halo_x_out[...] = ext_x[pl.ds(rows, HALO), :]
    halo_bc_out[...] = ext_bc[pl.ds(rows, HALO), :]
    halo_copies = [
        remote(halo_x_out, halo_x, halo_sems.at[0], halo_sems.at[1], "seq", seq_peer[1]),
        remote(halo_bc_out, halo_bc, halo_sems.at[2], halo_sems.at[3], "seq", seq_peer[1]),
    ]
    for copy in halo_copies:
        copy.start()
    for o in range(1, chips):
        convolve_rows(far_base(o), 1, chip_rows // 32)
    for block in range(1, chips):
        convolve_rows(block * chip_rows, 0, 1)

    head_of_lane = lax.broadcasted_iota(jnp.int32, (LANES, width), 1) // head_size
    spread = (
        (head_of_lane == lax.broadcasted_iota(jnp.int32, (LANES, width), 0)).astype(f32).astype(bf16)
    )
    spread_two = jnp.concatenate([spread, spread], axis=0)
    lower_tri = (
        lax.broadcasted_iota(jnp.int32, (SPAN, SPAN), 0)
        >= lax.broadcasted_iota(jnp.int32, (SPAN, SPAN), 1)
    ).astype(f32).astype(bf16)

    def spread_rows(value):
        return jnp.dot(
            jnp.concatenate(in_two(value), axis=1), spread_two, preferred_element_type=f32
        )

    def spread_exact(value):
        total = 0.0
        for part in in_three(value):
            total = total + jnp.dot(part, spread, preferred_element_type=f32)
        return total

    skip_wide = spread_exact(jnp.broadcast_to(small[2:3, :], (8, LANES)))[0:1]
    lasts = []
    for block in range(blocks):
        span = pl.ds(block * SPAN, SPAN)
        parts = jnp.dot(
            lower_tri, jnp.concatenate(in_three(dt_buf[span, :] * rate_row), axis=1),
            preferred_element_type=f32,
        )
        running = parts[:, :LANES] + parts[:, LANES : 2 * LANES] + parts[:, 2 * LANES :]
        cum_buf[span, :] = running
        lasts.append(running[SPAN - 1 : SPAN, :])

    for copy in halo_copies:
        copy.wait()
    first = me > 0
    ext_x[0:8, :] = jnp.where(first, halo_x[...], 0.0)
    ext_bc[0:8, :] = jnp.where(first, halo_bc[...], 0.0)
    convolve_rows(0, 0, 1)

    prefix = jnp.zeros((1, LANES), f32)
    prefixes = []
    for block in range(blocks):
        span = pl.ds(block * SPAN, SPAN)
        last = lasts[block]
        end_weight = spread_rows(jnp.exp(last - cum_buf[span, :]) * dt_buf[span, :])
        scaled = (conv_x[span, :].astype(f32) * end_weight).astype(bf16)
        new_state = lax.dot_general(
            conv_bc[span, pl.ds(0, state)], scaled, (((0,), (0,)), ((), ())),
            preferred_element_type=f32,
        )
        if block > 0:
            decay = spread_exact(jnp.broadcast_to(jnp.exp(last), (8, LANES)))[0:1]
            new_state = decay * states[block - 1] + new_state
        states[block] = new_state
        prefixes.append(prefix)
        prefix = prefix + last

    for j in range(devices):
        sum_out[j] = states[blocks - 1, pl.ds(j * share, share), :].astype(bf16)
    rate_out[...] = jnp.broadcast_to(prefix, (8, LANES))

    sum_copies, rate_copies = [], []
    for o in range(1, devices):
        sum_copies.append(
            remote(
                sum_out.at[seq_peer[o]], sum_in.at[o], sum_send.at[o], sum_recv.at[o],
                "seq", seq_peer[o],
            )
        )
        rate_copies.append(
            remote(
                rate_out, rate_in.at[o], rate_send.at[o], rate_recv.at[o], "seq", seq_peer[o]
            )
        )
    for a, b in zip(sum_copies, rate_copies):
        b.start()
        a.start()

    for o in range(max(chips - 1, 1), chips):
        far_gate(o, feeds - 1)

    row_index = lax.broadcasted_iota(jnp.int32, (LANES, LANES), 0)
    col_index = lax.broadcasted_iota(jnp.int32, (LANES, LANES), 1)
    causal = row_index >= col_index
    lane_index = lax.broadcasted_iota(jnp.int32, (SPAN, LANES), 1)
    pair = LANES // head_size

    def inside(block):
        span = pl.ds(pl.multiple_of(block * SPAN, SPAN), SPAN)
        running = cum_buf[span, :]
        running_t = running.T
        steps_t = dt_buf[span, :].T
        scores = lax.dot_general(
            conv_bc[span, pl.ds(state, state)], conv_bc[span, pl.ds(0, state)],
            (((1,), (1,)), ((), ())), preferred_element_type=f32,
        )
        half = SPAN // 2
        for strip in range(strips):
            lanes = pl.ds(strip * LANES, LANES)
            value = conv_x[span, lanes]
            upper, bottom, stacked_top, stacked = [], [], [], []
            for member in range(pair):
                head = strip * pair + member
                column = running[:, head : head + 1]
                line = running_t[head : head + 1, :]
                steps_line = steps_t[head : head + 1, :]

                def weights(r, c):
                    rs, cs = slice(r * half, (r + 1) * half), slice(c * half, (c + 1) * half)
                    gap = column[rs] - line[:, cs]
                    if r == c:
                        gap = jnp.where(causal, gap, -1e30)
                    return (scores[rs, cs] * jnp.exp(gap) * steps_line[:, cs]).astype(bf16)

                upper.append(weights(0, 0))
                bottom.extend([weights(1, 0), weights(1, 1)])
                mine = jnp.where(lane_index // head_size == member, value, jnp.zeros_like(value))
                stacked_top.append(mine[:half])
                stacked.append(mine)
            top_out = jnp.dot(
                jnp.concatenate(upper, axis=1), jnp.concatenate(stacked_top, axis=0),
                preferred_element_type=f32,
            )
            bottom_out = jnp.dot(
                jnp.concatenate(bottom, axis=1), jnp.concatenate(stacked, axis=0),
                preferred_element_type=f32,
            )
            both = jnp.concatenate([top_out, bottom_out], axis=0)
            y_buf[span, lanes] = both + skip_wide[:, strip * LANES : (strip + 1) * LANES] * value.astype(f32)

    early = max(blocks - 1, 1)

    def inside_step(block, carry):
        inside(block)
        return carry

    lax.fori_loop(0, early, inside_step, 0)

    for a, b in zip(sum_copies, rate_copies):
        b.wait()
        a.wait()
    sum_in[0] = sum_out[me]
    rate_in[0] = rate_out[...]

    running_state = jnp.zeros((share, width), f32)
    for i in range(devices):
        slot = lax.rem(me - i + devices, devices)
        carry_out[slot] = running_state.astype(bf16)
        decay = spread_exact(jnp.exp(rate_in[slot]))[0:1]
        running_state = decay * running_state + sum_in[slot].astype(f32)

    carry_copies = []
    for o in range(1, devices):
        carry_copies.append(
            remote(
                carry_out.at[o], carry_in.at[o], carry_send.at[o], carry_recv.at[o],
                "seq", seq_back[o],
            )
        )
    for copy in carry_copies:
        copy.start()
    lax.fori_loop(early, blocks, inside_step, 0)
    for o in range(chips):
        finish_gate(o * chip_rows)
    load_proj.wait()
    for copy in carry_copies:
        copy.wait()
    carry_in[0] = carry_out[0]
    for j in range(devices):
        slot = lax.rem(j - me + devices, devices)
        carried[pl.ds(j * share, share), :] = carry_in[slot].astype(f32)

    squares = []
    for block in range(blocks):
        span = pl.ds(block * SPAN, SPAN)
        entry_decay = spread_exact(jnp.broadcast_to(jnp.exp(prefixes[block]), (8, LANES)))[0:1]
        entering = entry_decay * carried[...]
        if block > 0:
            entering = entering + states[block - 1]
        entering = entering.astype(bf16)
        growth = jnp.concatenate(in_two(jnp.exp(cum_buf[span, :])), axis=1)
        partial_sum = jnp.zeros((SPAN, LANES), f32)
        for strip in range(strips):
            lanes = pl.ds(strip * LANES, LANES)
            column = slice(strip * LANES, (strip + 1) * LANES)
            cross = jnp.dot(
                conv_bc[span, pl.ds(state, state)], entering[:, column],
                preferred_element_type=f32,
            )
            scale = jnp.dot(growth, spread_two[:, column], preferred_element_type=f32)
            gated = (y_buf[span, lanes] + scale * cross) * gate[span, lanes]
            partial_sum = partial_sum + gated * gated
            normed[span, lanes] = (gated * norm_gain_ref[lanes].reshape(1, LANES)).astype(bf16)
        squares.append(jnp.sum(partial_sum.T, axis=0, keepdims=True))
    own_squares = jnp.concatenate(squares, axis=1)
    sq_out[...] = jnp.broadcast_to(own_squares, (8, rows))
    sq_copies = []
    for o in range(1, groups):
        sq_copies.append(
            remote(sq_out, sq_in.at[o], sq_send.at[o], sq_recv.at[o], "head", head_peer[o])
        )
    for copy in sq_copies:
        copy.start()

    pieces = proj.shape[1] // PIECE
    jobs = [(o, q) for o in list(range(1, chips)) + [0] for q in range(pieces)]

    def pair_copy(o, q):
        return remote(
            pair_out.at[o, q], pair_in.at[o, q], pair_send.at[o, q], pair_recv.at[o, q],
            "head", partner,
        )

    def chip_copy(o, q):
        target = lax.rem(chip + o, chips) * CORES + core
        return remote(
            chip_out.at[o - 1, q], chip_in.at[o - 1, q], chip_send.at[o, q], chip_recv.at[o, q],
            "head", target,
        )

    def product(o, q, whose):
        base = lax.rem(chip + o, chips) * CORES * own_rows
        here = pl.ds(pl.multiple_of(base + whose * own_rows, 16), own_rows)
        return jnp.dot(normed[here, :], proj[:, pl.ds(q * PIECE, PIECE)], preferred_element_type=f32)

    def start_job(o, q):
        pair_out[o, q] = product(o, q, 1 - core).astype(bf16)
        pair_copy(o, q).start()

    def finish_job(o, q):
        result = product(o, q, core)
        pair_copy(o, q).wait()
        result = result + pair_in[o, q].astype(f32)
        if o > 0:
            chip_out[o - 1, q] = result.astype(bf16)
            chip_copy(o, q).start()
        else:
            keep[q] = result

    for index, job in enumerate(jobs):
        start_job(*job)
        if index > 0:
            finish_job(*jobs[index - 1])
    finish_job(*jobs[-1])

    for copy in sq_copies:
        copy.wait()
    total = own_squares
    for o in range(1, groups):
        total = total + sq_in[o, 0:1, :]
    inverse = lax.rsqrt(total / total_width + norm_floor)
    for block in range(blocks):
        part = jnp.broadcast_to(inverse[:, block * SPAN : (block + 1) * SPAN], (LANES, SPAN)).T
        inv_col[pl.ds(block * SPAN, SPAN), :] = part
    own_inverse = inv_col[own, :]

    for q in range(pieces):
        result = keep[q]
        for o in range(1, chips):
            chip_copy(o, q).wait()
            result = result + chip_in[o - 1, q].astype(f32)
        for lower in range(0, PIECE, LANES):
            out_ref[:, pl.ds(q * PIECE + lower, LANES)] = (
                result[:, lower : lower + LANES] * own_inverse
            ).astype(bf16)

    for feed in range(feeds):
        mate_copy(0, feed).wait_send()
        for o in range(1, chips):
            row_copy(o, feed).wait_send()
            mate_copy(o, feed).wait_send()


def layer_call(*operands):
    tokens, _, inner_proj, outer_proj, kernel_x, kernel_bc, _, _, dt_bias, _, _, _, out_proj = operands
    devices, groups = lax.axis_size("seq"), lax.axis_size("head")
    own_rows, model = tokens.shape
    width, taps, state = kernel_x.shape[1], kernel_x.shape[0], kernel_bc.shape[1] // 2
    rows = own_rows * groups
    blocks, share = rows // SPAN, state // devices
    chips, strips, feeds = groups // CORES, width // LANES, model // FEED
    chip_rows = own_rows * CORES
    pieces = model // PIECE
    sizes = (devices, groups, rows, model, width, state, taps, dt_bias.shape[0])
    f32, bf16 = jnp.float32, jnp.bfloat16
    sem = pltpu.SemaphoreType.DMA
    vmem, hbm = pl.BlockSpec(memory_space=pltpu.VMEM), pl.BlockSpec(memory_space=pl.ANY)
    return pl.pallas_call(
        functools.partial(layer_kernel, sizes),
        out_shape=jax.ShapeDtypeStruct((own_rows, model), bf16),
        in_specs=[hbm, vmem, hbm, hbm] + [vmem] * 8 + [hbm],
        out_specs=vmem,
        scratch_shapes=[
            pltpu.VMEM((rows, model), bf16),
            pltpu.VMEM((own_rows, model), bf16),
            pltpu.VMEM((2, strips, DEPTH, 2, LANES), bf16),
            pltpu.VMEM((model, width), bf16),
            pltpu.VMEM((model, width), bf16),
            pltpu.VMEM(outer_proj.shape, bf16),
            pltpu.VMEM(out_proj.shape, bf16),
            pltpu.VMEM((rows, width), f32),
            pltpu.VMEM((rows + 8, width), f32),
            pltpu.VMEM((rows + 8, 2 * state), f32),
            pltpu.VMEM((rows, LANES), f32),
            pltpu.VMEM((HALO, width), f32),
            pltpu.VMEM((HALO, 2 * state), f32),
            pltpu.VMEM((HALO, width), f32),
            pltpu.VMEM((HALO, 2 * state), f32),
            pltpu.VMEM((rows, width), bf16),
            pltpu.VMEM((rows, 2 * state), bf16),
            pltpu.VMEM((rows, width), f32),
            pltpu.VMEM((rows, LANES), f32),
            pltpu.VMEM((blocks, state, width), f32),
            pltpu.VMEM((state, width), f32),
            pltpu.VMEM((devices, share, width), bf16),
            pltpu.VMEM((devices, share, width), bf16),
            pltpu.VMEM((8, LANES), f32),
            pltpu.VMEM((devices, 8, LANES), f32),
            pltpu.VMEM((devices, share, width), bf16),
            pltpu.VMEM((devices, share, width), bf16),
            pltpu.VMEM((rows, width), bf16),
            pltpu.VMEM((8, rows), f32),
            pltpu.VMEM((groups, 8, rows), f32),
            pltpu.VMEM((rows, LANES), f32),
            pltpu.VMEM((chips, pieces, own_rows, PIECE), bf16),
            pltpu.VMEM((chips, pieces, own_rows, PIECE), bf16),
            pltpu.VMEM((chips - 1, pieces, own_rows, PIECE), bf16),
            pltpu.VMEM((chips - 1, pieces, own_rows, PIECE), bf16),
            pltpu.VMEM((pieces, own_rows, PIECE), f32),
            pltpu.VMEM((8, LANES), f32),
            sem,
            sem((2, strips)),
            sem((2,)),
            sem((chips, feeds)),
            sem((chips, feeds)),
            sem((chips, feeds)),
            sem((chips, feeds)),
            sem((4,)),
            sem((devices,)),
            sem((devices,)),
            sem((devices,)),
            sem((devices,)),
            sem((devices,)),
            sem((devices,)),
            sem((groups,)),
            sem((groups,)),
            sem((chips, pieces)),
            sem((chips, pieces)),
            sem((chips, pieces)),
            sem((chips, pieces)),
        ],
        compiler_params=pltpu.CompilerParams(
            collective_id=0, has_side_effects=True, vmem_limit_bytes=67043328
        ),
    )(*operands)


def on_device(*args):
    operands = list(args)
    operands[3] = operands[3].T
    return layer_call(*operands)


def solution(mesh):
    return jax.shard_map(
        on_device,
        mesh=mesh,
        in_specs=(
            P(("seq", "head"), None),
            P(),
            P(None, None, "head"),
            P(),
            P(None, "head"),
            P(),
            P("head"),
            P(),
            P("head"),
            P("head"),
            P("head"),
            P("head"),
            P("head", None),
        ),
        out_specs=P(("seq", "head"), None),
        check_vma=False,
    )
```

time: 155 us -> 94.6 us (0.61)
  waiting for transfers between devices: 23 us -> 0 us
  matrix products: 19.6 us -> 0 us
  local copies, waits for them, and re-layouts: 19.1 us -> 2.21 us
  Pallas kernels: 76.2 us -> 92.2 us
  between operations: 13.5 us -> 0.01 us
  other arithmetic: 3.18 us -> 0 us
    all_gather x1 -> x0, waiting for transfers between devices: 22.3 us -> none  [on_device(): lax.all_gather(tokens, 'head', axis=0, tiled=True)]
    dot_general x2 -> x0, matrix products: 19.6 us -> none  [the longest x1 15.9 us: on_device(): jnp.dot(normed, joined_proj, preferred_element_type=jnp.float32)]
    pallas_call x1, Pallas kernels: 76.2 us -> 92.2 us  [layer_call(): pl.pallas_call(functools.partial(layer_kernel, sizes), out_shape=jax.Shap...]
    unnamed x18 -> x1, local copies, waits for them, and re-layouts: 15.8 us -> 2.21 us
    reduce_sum x1 -> x0, other arithmetic: 2.95 us -> none  [row_norm(): jnp.mean(widened * widened, axis=-1, keepdims=True) + norm_floor]
    broadcast_in_dim x4 -> x0, local copies, waits for them, and re-layouts: 1.85 us -> none  [the longest x1 0.6 us: on_device(): norm_gain[None]]
  transfers between devices with their start and end apart: 1 -> 0, of which waited for: 1 -> 0; matrix products, arithmetic and copies ran while one was open for 10% -> 0% of each run, Pallas kernels for 0% -> 0%
where the time goes in v1:
time: 94.6 us; the launch traced here: 94.4 us
  Pallas kernels  92.2 us (97%)
  local copies, waits for them, and re-layouts  2.21 us (2%)
    pallas_call x1, Pallas kernels, layer_call(): pl.pallas_call(functools.partial(layer_kernel, sizes), out_shape=jax.Shap...  92.2 us
    unnamed x1, local copies, waits for them, and re-layouts  2.21 us

profile of v1, /device:TPU:0, one launch (start us, length us, event | category | flops | bytes accessed | tf_op | source)
XLA Modules:
  0.0 94.4 jit_solution(7724615441973931216)
XLA Ops:
  0.0 92.2 %shard_map.127 = bf16[192,2560]{1,0:T(8,128)(2,1)} custom-call(bf16[192,2560]{1,0:T(8,128)(2,1)} %tokens_hbm.1, f32[2560]{0:T(1024)} %pre_gain_ref.1, bf16[2560,2,1280]{2,1,0:T(2,128)(2,1)} %inner_hbm.1, bf16[336,2560]{1,0:T(8,128)(2,1)} %bitcast.1, f32[4,1280]{1,0:T(4,128)} %kernel_x_ref.1, f32[4,256]{1,0:T(4,128)} %kernel_bc_ref.1, f32[1280]{0:T(1024)} %offset_x_ref.1, ...), custom_call_target="tpu_custom_call" | custom-call | tf_op jit(solution)/shard_map/pallas_call | solution.py:674
  92.2 2.2 %copy.15 = bf16[192,2560]{1,0:T(8,128)(2,1)} copy(bf16[192,2560]{1,0:T(8,128)(2,1)} %shard_map.127) | data formatting | bytes 1966080

commit v2 on v1

--- a/solution.py
+++ b/solution.py
@@ -88,6 +88,7 @@
     sq_out,
     sq_in,
     inv_col,
+    entered,
     pair_out,
     pair_in,
     chip_out,
@@ -172,7 +173,6 @@
 
     def clear(k, carry):
         row = pl.multiple_of(k * 64, 64)
-        gate[pl.ds(row, 64), :] = jnp.zeros((64, width), f32)
         ext_x[pl.ds(8 + row, 64), :] = jnp.zeros((64, width), f32)
         ext_bc[pl.ds(8 + row, 64), :] = jnp.zeros((64, 2 * state), f32)
         dt_buf[pl.ds(row, 64), :] = jnp.zeros((64, LANES), f32)
@@ -284,7 +284,6 @@
         begin = pl.multiple_of(step * DEPTH, DEPTH)
         gather_into(ext_x, 8, local_base, inner_w, begin, DEPTH)
         gather_outer(local_base, begin, DEPTH)
-        gather_into(gate, 0, local_base, gate_w, begin, DEPTH)
         return carry
 
     lax.fori_loop(0, steps, local_step, 0)
@@ -307,15 +306,12 @@
 
         lax.fori_loop(0, chip_rows // 32, step, 0)
 
-    def finish_gate(base):
-        def step(k, carry):
-            here = pl.ds(pl.multiple_of(base + k * 32, 32), 32)
-            for column in range(0, width, LANES):
-                lanes = pl.ds(column, LANES)
-                gate[here, lanes] = silu(gate[here, lanes].astype(bf16).astype(f32))
-            return carry
-
-        lax.fori_loop(0, chip_rows // 32, step, 0)
+    def fill_gate(base, size):
+        here = pl.ds(pl.multiple_of(base, 16), size)
+        for column in range(0, width, tile):
+            columns = pl.ds(column, tile)
+            gate_in = jnp.dot(tok[here, :], gate_w[:, columns], preferred_element_type=f32)
+            gate[here, columns] = silu(gate_in.astype(bf16).astype(f32))
 
     def convolve(source, weight, bias, target, columns, row):
         for lower in range(0, columns, LANES):
@@ -352,23 +348,17 @@
         gather_into(ext_x, 8, far_base(o), inner_w, begin, FEED)
         gather_outer(far_base(o), begin, FEED)
 
-    def far_gate(o, feed):
-        gather_into(gate, 0, far_base(o), gate_w, pl.multiple_of(feed * FEED, FEED), FEED)
-
     for o in range(1, chips):
         take_feed(o, 0)
 
         def far_loop(feed, carry):
             take_feed(o, feed + 1)
             far_step(o, feed)
-            far_gate(o, feed)
             return carry
 
         lax.fori_loop(0, feeds - 1, far_loop, 0)
         far_step(o, feeds - 1)
         finish_rows(far_base(o))
-        if o < chips - 1:
-            far_gate(o, feeds - 1)
 
     halo_x_out[...] = ext_x[pl.ds(rows, HALO), :]
     halo_bc_out[...] = ext_bc[pl.ds(rows, HALO), :]
@@ -462,8 +452,11 @@
         b.start()
         a.start()
 
-    for o in range(max(chips - 1, 1), chips):
-        far_gate(o, feeds - 1)
+    def gate_step(block, carry):
+        fill_gate(block * SPAN, SPAN)
+        return carry
+
+    lax.fori_loop(0, blocks, gate_step, 0)
 
     row_index = lax.broadcasted_iota(jnp.int32, (LANES, LANES), 0)
     col_index = lax.broadcasted_iota(jnp.int32, (LANES, LANES), 1)
@@ -514,13 +507,9 @@
             both = jnp.concatenate([top_out, bottom_out], axis=0)
             y_buf[span, lanes] = both + skip_wide[:, strip * LANES : (strip + 1) * LANES] * value.astype(f32)
 
-    early = max(blocks - 1, 1)
-
     def inside_step(block, carry):
         inside(block)
         return carry
-
-    lax.fori_loop(0, early, inside_step, 0)
 
     for a, b in zip(sum_copies, rate_copies):
         b.wait()
@@ -545,9 +534,7 @@
         )
     for copy in carry_copies:
         copy.start()
-    lax.fori_loop(early, blocks, inside_step, 0)
-    for o in range(chips):
-        finish_gate(o * chip_rows)
+    lax.fori_loop(0, blocks, inside_step, 0)
     load_proj.wait()
     for copy in carry_copies:
         copy.wait()
@@ -556,37 +543,44 @@
         slot = lax.rem(j - me + devices, devices)
         carried[pl.ds(j * share, share), :] = carry_in[slot].astype(f32)
 
-    squares = []
     for block in range(blocks):
-        span = pl.ds(block * SPAN, SPAN)
         entry_decay = spread_exact(jnp.broadcast_to(jnp.exp(prefixes[block]), (8, LANES)))[0:1]
         entering = entry_decay * carried[...]
         if block > 0:
             entering = entering + states[block - 1]
-        entering = entering.astype(bf16)
+        entered[block] = entering.astype(bf16)
+
+    unit = chip_rows // 3 if chip_rows % 3 == 0 and SPAN % (chip_rows // 3) == 0 else 64
+
+    def cross_unit(base):
+        span = pl.ds(pl.multiple_of(base, 16), unit)
+        block = base // SPAN
         growth = jnp.concatenate(in_two(jnp.exp(cum_buf[span, :])), axis=1)
-        partial_sum = jnp.zeros((SPAN, LANES), f32)
-        for strip in range(strips):
-            lanes = pl.ds(strip * LANES, LANES)
-            column = slice(strip * LANES, (strip + 1) * LANES)
+        partial_sum = jnp.zeros((unit, LANES), f32)
+        for column in range(0, width, tile):
+            lanes = pl.ds(column, tile)
             cross = jnp.dot(
-                conv_bc[span, pl.ds(state, state)], entering[:, column],
+                conv_bc[span, pl.ds(state, state)], entered[block, :, lanes],
                 preferred_element_type=f32,
             )
-            scale = jnp.dot(growth, spread_two[:, column], preferred_element_type=f32)
+            scale = jnp.dot(
+                growth, spread_two[:, column : column + tile], preferred_element_type=f32
+            )
             gated = (y_buf[span, lanes] + scale * cross) * gate[span, lanes]
-            partial_sum = partial_sum + gated * gated
-            normed[span, lanes] = (gated * norm_gain_ref[lanes].reshape(1, LANES)).astype(bf16)
-        squares.append(jnp.sum(partial_sum.T, axis=0, keepdims=True))
-    own_squares = jnp.concatenate(squares, axis=1)
-    sq_out[...] = jnp.broadcast_to(own_squares, (8, rows))
-    sq_copies = []
-    for o in range(1, groups):
-        sq_copies.append(
-            remote(sq_out, sq_in.at[o], sq_send.at[o], sq_recv.at[o], "head", head_peer[o])
-        )
-    for copy in sq_copies:
-        copy.start()
+            squared = gated * gated
+            for lower in range(0, tile, LANES):
+                partial_sum = partial_sum + squared[:, lower : lower + LANES]
+            normed[span, lanes] = (gated * norm_gain_ref[lanes].reshape(1, tile)).astype(bf16)
+        inv_col[span, :] = partial_sum
+
+    def cross_chip(o):
+        base = lax.rem(chip + o, chips) * chip_rows
+
+        def step(k, carry):
+            cross_unit(base + k * unit)
+            return carry
+
+        lax.fori_loop(0, chip_rows // unit, step, 0)
 
     pieces = proj.shape[1] // PIECE
     jobs = [(o, q) for o in list(range(1, chips)) + [0] for q in range(pieces)]
@@ -623,7 +617,31 @@
         else:
             keep[q] = result
 
+    def send_squares():
+        own_squares = jnp.concatenate(
+            [
+                jnp.sum(inv_col[pl.ds(block * SPAN, SPAN), :].T, axis=0, keepdims=True)
+                for block in range(blocks)
+            ],
+            axis=1,
+        )
+        sq_out[...] = own_squares
+        copies = [
+            remote(sq_out, sq_in.at[o], sq_send.at[o], sq_recv.at[o], "head", head_peer[o])
+            for o in range(1, groups)
+        ]
+        for copy in copies:
+            copy.start()
+        return own_squares, copies
+
+    cross_chip(1)
     for index, job in enumerate(jobs):
+        o, q = job
+        if q == 0 and 1 < o:
+            cross_chip(o)
+        if q == 0 and o == 0:
+            cross_chip(0)
+            own_squares, sq_copies = send_squares()
         start_job(*job)
         if index > 0:
             finish_job(*jobs[index - 1])
@@ -633,7 +651,7 @@
         copy.wait()
     total = own_squares
     for o in range(1, groups):
-        total = total + sq_in[o, 0:1, :]
+        total = total + sq_in[o]
     inverse = lax.rsqrt(total / total_width + norm_floor)
     for block in range(blocks):
         part = jnp.broadcast_to(inverse[:, block * SPAN : (block + 1) * SPAN], (LANES, SPAN)).T
@@ -705,9 +723,10 @@
             pltpu.VMEM((devices, share, width), bf16),
             pltpu.VMEM((devices, share, width), bf16),
             pltpu.VMEM((rows, width), bf16),
-            pltpu.VMEM((8, rows), f32),
-            pltpu.VMEM((groups, 8, rows), f32),
+            pltpu.VMEM((1, rows), f32),
+            pltpu.VMEM((groups, 1, rows), f32),
             pltpu.VMEM((rows, LANES), f32),
+            pltpu.VMEM((blocks, state, width), bf16),
             pltpu.VMEM((chips, pieces, own_rows, PIECE), bf16),
             pltpu.VMEM((chips, pieces, own_rows, PIECE), bf16),
             pltpu.VMEM((chips - 1, pieces, own_rows, PIECE), bf16),

time: 94.6 us -> 89 us (0.941)
  Pallas kernels: 92.2 us -> 86.6 us
    pallas_call x1, Pallas kernels: 92.2 us -> 86.6 us  [layer_call(): pl.pallas_call(functools.partial(layer_kernel, sizes), out_shape=jax.Shap...]
where the time goes in v2:
time: 89 us; the launch traced here: 88.8 us
  Pallas kernels  86.6 us (97%)
  local copies, waits for them, and re-layouts  2.21 us (2%)
    pallas_call x1, Pallas kernels, layer_call(): pl.pallas_call(functools.partial(layer_kernel, sizes), out_shape=jax.Shap...  86.6 us
    unnamed x1, local copies, waits for them, and re-layouts  2.21 us

profile of v2, /device:TPU:0, one launch (start us, length us, event | category | flops | bytes accessed | tf_op | source)
XLA Modules:
  0.0 88.8 jit_solution(14202948030452233760)
XLA Ops:
  0.0 86.6 %shard_map.127 = bf16[192,2560]{1,0:T(8,128)(2,1)} custom-call(bf16[192,2560]{1,0:T(8,128)(2,1)} %tokens_hbm.1, f32[2560]{0:T(1024)} %pre_gain_ref.1, bf16[2560,2,1280]{2,1,0:T(2,128)(2,1)} %inner_hbm.1, bf16[336,2560]{1,0:T(8,128)(2,1)} %bitcast.1, f32[4,1280]{1,0:T(4,128)} %kernel_x_ref.1, f32[4,256]{1,0:T(4,128)} %kernel_bc_ref.1, f32[1280]{0:T(1024)} %offset_x_ref.1, ...), custom_call_target="tpu_custom_call" | custom-call | tf_op jit(solution)/shard_map/pallas_call | solution.py:692
  86.6 2.2 %copy.15 = bf16[192,2560]{1,0:T(8,128)(2,1)} copy(bf16[192,2560]{1,0:T(8,128)(2,1)} %shard_map.127) | data formatting | bytes 1966080

commit v3 on v2

--- a/solution.py
+++ b/solution.py
@@ -10,10 +10,11 @@
 SPAN = 256
 HALO = 8
 LANES = 128
-PIECE = 512
+PIECE = 256
 CORES = 2
-FEED = 512
+FEED = 256
 DEPTH = 256
+SLOTS = 4
 
 norm_floor = 0.1
 
@@ -156,8 +157,9 @@
         raw_copy(0, 0, strip).start()
     load_outer = pltpu.make_async_copy(outer_hbm, outer_w, load_sems.at[0])
     load_outer.start()
-    for strip in range(strips):
-        raw_copy(1, 1, strip).start()
+    for slot in range(1, SLOTS):
+        for strip in range(strips):
+            raw_copy(slot, slot, strip).start()
     load_proj = pltpu.make_async_copy(proj_hbm, proj, load_sems.at[1])
 
     barrier = pltpu.get_barrier_semaphore()
@@ -178,23 +180,27 @@
         dt_buf[pl.ds(row, 64), :] = jnp.zeros((64, LANES), f32)
         return carry
 
+    group_rows = 48 if own_rows % 48 == 0 else 16
+
     def normalise(k, carry):
-        row = pl.multiple_of(k * 16, 16)
-        squares = jnp.zeros((16, LANES), f32)
+        row = pl.multiple_of(k * group_rows, 16)
+        here = pl.ds(row, group_rows)
+        squares = jnp.zeros((group_rows, LANES), f32)
         for column in range(0, model, LANES):
-            value = tok_in[pl.ds(row, 16), pl.ds(column, LANES)].astype(f32)
+            value = tok_in[here, pl.ds(column, LANES)].astype(f32)
             squares = squares + value * value
         inverse = lax.rsqrt(jnp.sum(squares, axis=1, keepdims=True) / model + norm_floor)
+        there = pl.ds(pl.multiple_of(group * own_rows + row, 16), group_rows)
         for column in range(0, model, LANES):
             lanes = pl.ds(column, LANES)
-            value = tok_in[pl.ds(row, 16), lanes].astype(f32)
-            tok[pl.ds(pl.multiple_of(group * own_rows + row, 16), 16), lanes] = (
+            value = tok_in[here, lanes].astype(f32)
+            tok[there, lanes] = (
                 value * inverse * pre_gain_ref[lanes].reshape(1, LANES)
             ).astype(bf16)
         return carry
 
     load_tok.wait()
-    lax.fori_loop(0, own_rows // 16, normalise, 0)
+    lax.fori_loop(0, own_rows // group_rows, normalise, 0)
     pl.semaphore_wait(barrier, devices + groups - 2)
 
     def feed_at(chip_index, core_index, feed):
@@ -266,27 +272,36 @@
     local_base = pl.multiple_of(chip * chip_rows, 32)
     load_outer.wait()
 
-    def local_step(step, carry):
-        slot = lax.rem(step, 2)
+    def wait_raw(step, slot):
         for strip in range(strips):
             raw_copy(step, slot, strip).wait()
-        separate(step, slot)
-
-        @pl.when(step + 2 < steps)
-        def _():
-            for strip in range(strips):
-                raw_copy(step + 2, slot, strip).start()
-
-        @pl.when(lax.rem(step, FEED // DEPTH) == 0)
-        def _():
-            mate_copy(0, step // (FEED // DEPTH)).wait_recv()
-
+
+    def local_product(step):
         begin = pl.multiple_of(step * DEPTH, DEPTH)
         gather_into(ext_x, 8, local_base, inner_w, begin, DEPTH)
         gather_outer(local_base, begin, DEPTH)
+
+    def local_step(step, carry):
+        slot = lax.rem(step, SLOTS)
+        wait_raw(step, slot)
+        mate_copy(0, step - 1).wait_recv()
+        local_product(step - 1)
+        separate(step, slot)
+
+        @pl.when(step + SLOTS < steps)
+        def _():
+            for strip in range(strips):
+                raw_copy(step + SLOTS, slot, strip).start()
+
         return carry
 
-    lax.fori_loop(0, steps, local_step, 0)
+    wait_raw(0, 0)
+    separate(0, 0)
+    for strip in range(strips):
+        raw_copy(SLOTS, 0, strip).start()
+    lax.fori_loop(1, steps, local_step, 0)
+    mate_copy(0, steps - 1).wait_recv()
+    local_product(steps - 1)
     load_proj.start()
 
     bias_row, rate_row = small[0:1, :], small[1:2, :]
@@ -697,7 +712,7 @@
         scratch_shapes=[
             pltpu.VMEM((rows, model), bf16),
             pltpu.VMEM((own_rows, model), bf16),
-            pltpu.VMEM((2, strips, DEPTH, 2, LANES), bf16),
+            pltpu.VMEM((SLOTS, strips, DEPTH, 2, LANES), bf16),
             pltpu.VMEM((model, width), bf16),
             pltpu.VMEM((model, width), bf16),
             pltpu.VMEM(outer_proj.shape, bf16),
@@ -734,7 +749,7 @@
             pltpu.VMEM((pieces, own_rows, PIECE), f32),
             pltpu.VMEM((8, LANES), f32),
             sem,
-            sem((2, strips)),
+            sem((SLOTS, strips)),
             sem((2,)),
             sem((chips, feeds)),
             sem((chips, feeds)),

time: 89 us -> 90 us (1.011)
  Pallas kernels: 86.6 us -> 87.5 us
    pallas_call x1, Pallas kernels: 86.6 us -> 87.5 us  [layer_call(): pl.pallas_call(functools.partial(layer_kernel, sizes), out_shape=jax.Shap...]
where the time goes in v3:
time: 90 us; the launch traced here: 89.8 us
  Pallas kernels  87.5 us (97%)
  local copies, waits for them, and re-layouts  2.21 us (2%)
    pallas_call x1, Pallas kernels, layer_call(): pl.pallas_call(functools.partial(layer_kernel, sizes), out_shape=jax.Shap...  87.5 us
    unnamed x1, local copies, waits for them, and re-layouts  2.21 us

profile of v3, /device:TPU:0, one launch (start us, length us, event | category | flops | bytes accessed | tf_op | source)
XLA Modules:
  0.0 89.8 jit_solution(11544696849627368264)
XLA Ops:
  0.0 87.5 %shard_map.127 = bf16[192,2560]{1,0:T(8,128)(2,1)} custom-call(bf16[192,2560]{1,0:T(8,128)(2,1)} %tokens_hbm.1, f32[2560]{0:T(1024)} %pre_gain_ref.1, bf16[2560,2,1280]{2,1,0:T(2,128)(2,1)} %inner_hbm.1, bf16[336,2560]{1,0:T(8,128)(2,1)} %bitcast.1, f32[4,1280]{1,0:T(4,128)} %kernel_x_ref.1, f32[4,256]{1,0:T(4,128)} %kernel_bc_ref.1, f32[1280]{0:T(1024)} %offset_x_ref.1, ...), custom_call_target="tpu_custom_call" | custom-call | tf_op jit(solution)/shard_map/pallas_call | solution.py:707
  87.6 2.2 %copy.15 = bf16[192,2560]{1,0:T(8,128)(2,1)} copy(bf16[192,2560]{1,0:T(8,128)(2,1)} %shard_map.127) | data formatting | bytes 1966080
